TPU v7x, 32 devices: a whole 2x2x4 slice. The times are simulated.
32 devices in a mesh: block: 4 (over x, core), span: 4 (over z), model: 2 (over y).
Axes of the slice: x: 2, y: 2, z: 4, core: 2. Of those that a mesh axis runs over, the one named last changes fastest.
Arguments:
- fresh_keys: bfloat16 [16, 8192, 8, 128], P(None, ('block', 'span'), 'model'), may hold values from -6 to 6
- fresh_values: bfloat16 [16, 8192, 8, 128], P(None, ('block', 'span'), 'model'), may hold values from -6 to 6
- turn_angle: float32 [8192, 64], replicated, may hold values from -3.140625 to 3.140625
Outputs:
- decode_keys: bfloat16 [16, 8, 128, 8192], P(('block', 'span'), 'model')
- decode_values: bfloat16 [16, 8192, 8, 128], P(('block', 'span'), None, 'model')
- page_high: bfloat16 [16, 128, 8, 128], P(('block', 'span'), None, 'model')
- page_low: bfloat16 [16, 128, 8, 128], P(('block', 'span'), None, 'model')
All inputs are finite; a program needn't handle non-finite values.
Results may differ from a plain program's by a relative error of at most 0.001.
Values may be sent and summed in bfloat16 or wider, within the bound.
A program may use at most 128 MiB of HBM per device.

v0:
```python
import jax
import jax.numpy as jnp
from jax import lax
from jax.sharding import PartitionSpec as P

PAGE = 64


def apply_rotary(vectors, angle):
    half = vectors.shape[-1] // 2
    cosine, sine = (jnp.cos(angle)[None, :, None, :], jnp.sin(angle)[None, :, None, :])
    first, second = (vectors[..., :half], vectors[..., half:])
    return jnp.concatenate(
        [first * cosine - second * sine, second * cosine + first * sine], axis=-1
    )


def ready_to_store(plain_keys, angle):
    wide_keys = plain_keys.astype(jnp.float32)
    return apply_rotary(wide_keys, angle)


def body(fresh_keys, fresh_values, turn_angle):
    my_angles = lax.dynamic_slice_in_dim(
        turn_angle, lax.axis_index(("block", "span")) * fresh_keys.shape[1], fresh_keys.shape[1]
    )
    sent_keys = ready_to_store(fresh_keys, my_angles).astype(jnp.bfloat16)
    moved_keys, decode_values = (
        lax.all_to_all(sent_keys, ("block", "span"), split_axis=0, concat_axis=1, tiled=True),
        lax.all_to_all(fresh_values, ("block", "span"), split_axis=0, concat_axis=1, tiled=True),
    )
    page_view = moved_keys.reshape(
        moved_keys.shape[0], -1, PAGE, moved_keys.shape[2], moved_keys.shape[3]
    )
    page_high = jnp.max(page_view, axis=2)
    page_low = jnp.min(page_view, axis=2)
    decode_keys = jnp.transpose(moved_keys, (0, 2, 3, 1))
    return (decode_keys, decode_values, page_high, page_low)


def solution(mesh):
    placed = (
        P(None, ("block", "span"), "model", None),
        P(None, ("block", "span"), "model", None),
        P(),
    )
    return jax.shard_map(
        body,
        mesh=mesh,
        in_specs=placed,
        out_specs=(
            P(("block", "span"), "model", None, None),
            P(("block", "span"), None, "model", None),
            P(("block", "span"), None, "model", None),
            P(("block", "span"), None, "model", None),
        ),
        check_vma=False,
    )
```

profile of v0, /device:TPU:9, one launch (start us, length us, event | category | flops | bytes accessed | tf_op | source)
XLA Modules:
  0.0 413.9 jit_solution(11221866299321487730)
XLA Ops:
  0.6 1.4 dynamic-slice_cosine_fusion
  2.0 0.1 copy.7
  2.1 0.1 copy.8
  2.3 4.7 %convert_element_type.4 = f32[16,512,4,128]{3,2,1,0:T(4,128)S(1)} convert(bf16[16,512,4,128]{3,2,1,0:T(4,128)(2,1)} %param.3) | non-fusion elementwise | flops 4194304 | bytes 25165824 | tf_op jit(solution)/shard_map/convert_element_type | solution.py:19
  7.0 11.6 %subtract_convert_fusion = (bf16[16,512,4,64]{3,2,1,0:T(4,128)(2,1)S(1)}, bf16[16,512,4,64]{3,2,1,0:T(4,128)(2,1)S(1)}) fusion(f32[16,512,4,128]{3,2,1,0:T(4,128)S(1)} %convert_element_type.4, f32[512,64]{1,0:T(8,128)S(1)} %copy.8, f32[512,64]{1,0:T(8,128)S(1)} %copy.7), kind=kLoop, calls=%fused_computation.1 | loop fusion | flops 16777216 | bytes 25427968 | tf_op jit(solution)/shard_map/convert
  18.6 11.5 %pad_maximum_fusion = bf16[16,512,4,128]{3,2,1,0:T(4,128)(2,1)S(1)} fusion(bf16[16,512,4,64]{3,2,1,0:T(4,128)(2,1)S(1)} %get-tuple-element.7, bf16[16,512,4,64]{3,2,1,0:T(4,128)(2,1)S(1)} %get-tuple-element.6), kind=kLoop, calls=%fused_computation.2 | loop fusion | flops 16777216 | bytes 16777216 | tf_op jit(solution)/shard_map/concatenate | solution.py:13
  30.1 188.8 %all_to_all.24 = bf16[16,512,4,128]{3,2,1,0:T(4,128)(2,1)} all-to-all(bf16[16,512,4,128]{3,2,1,0:T(4,128)(2,1)S(1)} %pad_maximum_fusion), channel_id=1, replica_groups=mesh['block'=4,'span'=4,'model'=2] {'block','span'}, dimensions={0} | all-to-all | bytes 16777216 | tf_op jit(solution)/shard_map/all_to_all | solution.py:29
  218.9 6.5 %all-to-all-start.1 = ((bf16[16,512,4,128]{3,2,1,0:T(4,128)(2,1)}), bf16[16,512,4,128]{3,2,1,0:T(4,128)(2,1)}, u32[]{:S(2)}, u32[]{:S(2)}) async-start(bf16[16,512,4,128]{3,2,1,0:T(4,128)(2,1)} %param.4), calls=%async_computation.1 | async-start | bytes 16777216 | tf_op jit(solution)/shard_map/all_to_all | solution.py:30
  225.4 13.6 %copy.10 = bf16[1,8192,4,128]{1,3,2,0:T(8,128)(2,1)} copy(bf16[1,8192,4,128]{3,2,1,0:T(4,128)(2,1)} %bitcast.6) | data formatting | bytes 16777216 | tf_op jit(solution)/shard_map/all_to_all | solution.py:29
  239.0 18.3 %fusion = (bf16[128,4,128]{2,1,0:T(4,128)(2,1)}, bf16[128,4,128]{2,1,0:T(4,128)(2,1)}) fusion(bf16[1,128,64,4,128]{4,3,2,1,0:T(4,128)(2,1)} %bitcast.7), kind=kLoop, calls=%fused_computation.5 | loop fusion | flops 8257536 | bytes 8650752 | tf_op jit(solution)/shard_map/reduce_min | solution.py:36
  257.4 148.4 %all-to-all-done.1 = bf16[16,512,4,128]{3,2,1,0:T(4,128)(2,1)} async-done(((bf16[16,512,4,128]{3,2,1,0:T(4,128)(2,1)}), bf16[16,512,4,128]{3,2,1,0:T(4,128)(2,1)}, u32[]{:S(2)}, u32[]{:S(2)}) %all-to-all-start.1) | async-done | bytes 8388640 | tf_op jit(solution)/shard_map/all_to_all | solution.py:30
  405.8 8.1 %copy.12 = bf16[1,8192,4,128]{3,2,1,0:T(4,128)(2,1)} copy(bf16[1,8192,4,128]{3,2,1,0:T(4,128)(2,1)} %bitcast.2) | data formatting | bytes 16777216
Async XLA Ops:
  218.9 186.9 %all-to-all-start.1 = ((bf16[16,512,4,128]{3,2,1,0:T(4,128)(2,1)}), bf16[16,512,4,128]{3,2,1,0:T(4,128)(2,1)}, u32[]{:S(2)}, u32[]{:S(2)}) async-start(bf16[16,512,4,128]{3,2,1,0:T(4,128)(2,1)} %param.4), calls=%async_computation.1 | async-start | bytes 16777216 | tf_op jit(solution)/shard_map/all_to_all | solution.py:30
where the time goes:
time: 419 us; the launch traced here: 414 us
  blocking collectives  189 us (45%)
  waiting for transfers between devices  148 us (35%)
  other arithmetic  46.1 us (11%)
  local copies, waits for them, and re-layouts  23.3 us (6%)
  starting transfers between devices  6.51 us (2%)
    all_to_all x1, blocking collectives, body(): lax.all_to_all(sent_keys, ('block', 'span'), split_axis=0, concat_axis=1,...  189 us
    all_to_all x1, waiting for transfers between devices, body(): lax.all_to_all(fresh_values, ('block', 'span'), split_axis=0, concat_axis...  148 us
    reduce_min x1, other arithmetic, body(): page_low = jnp.min(page_view, axis=2)  18.3 us
    all_to_all x1, local copies, waits for them, and re-layouts, body(): lax.all_to_all(sent_keys, ('block', 'span'), split_axis=0, concat_axis=1,...  13.6 us
    another operation x1, other arithmetic  11.6 us
    concatenate x1, other arithmetic, apply_rotary(): jnp.concatenate([first * cosine - second * sine, second * cosine + first...  11.5 us
  transfers between devices with their start and end apart: 1, of which 1 were waited for; matrix products, arithmetic and copies ran while one was open for 8% of the time, Pallas kernels for 0%

commit v1 on v0

v1 whole, which is shorter than its diff:
```python
import functools

import jax
import jax.numpy as jnp
from jax import lax
from jax.experimental import pallas as pl
from jax.experimental.pallas import tpu as pltpu
from jax.sharding import PartitionSpec as P

PAGE = 64
ROWS = 256


def kernel(
    dims, keys, values, angle,
    out_keys, out_values, out_high, out_low,
    held, landed, wide, cosine, sine, turn, staged, bounds, own,
    send_v, recv_v, send_k, recv_k, load_sem, own_sem, stage_sem,
):
    spans, n, seqs, length, heads, size = dims
    rows = length * heads
    pages = length // PAGE
    block, span, model = (lax.axis_index(a) for a in ("block", "span", "model"))
    me = block * spans + span

    def peer(j):
        return (j // spans, lax.rem(j, spans), model)

    def send_values(j):
        return pltpu.make_async_remote_copy(
            src_ref=values.at[pl.ds(j * seqs, seqs)],
            dst_ref=out_values.at[:, me],
            send_sem=send_v.at[j],
            recv_sem=recv_v.at[me],
            device_id=peer(j),
            device_id_type=pl.DeviceIdType.MESH,
        )

    def recv_values(j):
        return pltpu.make_async_remote_copy(
            src_ref=values.at[pl.ds(j * seqs, seqs)],
            dst_ref=out_values.at[:, j],
            send_sem=send_v.at[j],
            recv_sem=recv_v.at[j],
            device_id=peer(j),
            device_id_type=pl.DeviceIdType.MESH,
        )

    def send_keys(j):
        return pltpu.make_async_remote_copy(
            src_ref=held.at[pl.ds(j * seqs, seqs)],
            dst_ref=landed.at[pl.ds(me * seqs, seqs)],
            send_sem=send_k.at[j],
            recv_sem=recv_k.at[me],
            device_id=peer(j),
            device_id_type=pl.DeviceIdType.MESH,
        )

    def recv_keys(j):
        return pltpu.make_async_remote_copy(
            src_ref=held.at[pl.ds(j * seqs, seqs)],
            dst_ref=landed.at[pl.ds(j * seqs, seqs)],
            send_sem=send_k.at[j],
            recv_sem=recv_k.at[j],
            device_id=peer(j),
            device_id_type=pl.DeviceIdType.MESH,
        )

    load_keys = pltpu.make_async_copy(keys, held, load_sem.at[0])
    load_angle = pltpu.make_async_copy(
        angle.at[:, pl.ds(pl.multiple_of(me * length, length), length)], turn, load_sem.at[1]
    )
    load_own = pltpu.make_async_copy(values.at[pl.ds(me * seqs, seqs)], own, own_sem.at[0])
    keep_own = pltpu.make_async_copy(own, out_values.at[:, me], own_sem.at[1])
    load_angle.start()
    load_keys.start()
    load_own.start()

    barrier = pltpu.get_barrier_semaphore()

    @pl.loop(1, n)
    def _(k):
        pl.semaphore_signal(
            barrier, inc=1, device_id=peer(lax.rem(me + k, n)),
            device_id_type=pl.DeviceIdType.MESH,
        )

    pl.semaphore_wait(barrier, n - 1)

    @pl.loop(1, n)
    def _(k):
        send_values(lax.rem(me + k, n)).start()

    load_angle.wait()
    c, s = jnp.cos(turn[...]), jnp.sin(turn[...])
    wide_c = jnp.concatenate([c, c], axis=0).T
    wide_s = jnp.concatenate([-s, s], axis=0).T
    for h in range(heads):
        cosine[pl.ds(h, length, stride=heads), :] = wide_c
        sine[pl.ds(h, length, stride=heads), :] = wide_s
    load_own.wait()
    keep_own.start()
    load_keys.wait()

    def rotate(j):
        for q in range(seqs):

            @pl.loop(0, rows // ROWS)
            def _(r):
                at = pl.ds(pl.multiple_of(r * ROWS, ROWS), ROWS)
                x = held[j * seqs + q, at, :].astype(jnp.float32)
                y = x * cosine[at, :] + pltpu.roll(x, size // 2, 1) * sine[at, :]
                held[j * seqs + q, at, :] = y.astype(jnp.bfloat16)

    rotate(lax.rem(me + 1, n))

    @pl.loop(2, n + 1)
    def _(k):
        rotate(lax.rem(me + k, n))
        send_keys(lax.rem(me + k - 1, n)).start()

    keep_own.wait()

    def stage(j, q, slot):
        return pltpu.make_async_copy(
            staged.at[slot],
            out_keys.at[q, :, :, pl.ds(pl.multiple_of(j * length, length), length)],
            stage_sem.at[slot],
        )

    def finish(ref, row, j, q, slot, first):
        wide[...] = ref[row].astype(jnp.float32)

        @pl.when(jnp.logical_not(first))
        def _():
            stage(j, q, slot).wait()

        for h in range(heads):
            part = wide[pl.ds(h, length, stride=heads), :]
            staged[slot, h] = part.T.astype(jnp.bfloat16)
            grouped = part.reshape(pages, PAGE, size)
            bounds[0, pl.ds(h, pages, stride=heads), :] = jnp.max(grouped, axis=1)
            bounds[1, pl.ds(h, pages, stride=heads), :] = jnp.min(grouped, axis=1)
        out_high[q, j] = bounds[0].astype(jnp.bfloat16)
        out_low[q, j] = bounds[1].astype(jnp.bfloat16)
        stage(j, q, slot).start()

    total = n * seqs
    for q in range(seqs):
        finish(held, me * seqs + q, me, q, q % 2, jnp.bool_(q < 2))

    @pl.loop(1, n)
    def _(k):
        j = lax.rem(me + n - k, n)
        recv_keys(j).wait_recv()
        for q in range(seqs):
            step = k * seqs + q
            finish(landed, j * seqs + q, j, q, lax.rem(step, 2), step < 2)

    for last in range(max(0, total - 2), total):
        stage(0, 0, last % 2).wait()

    @pl.loop(1, n)
    def _(k):
        j = lax.rem(me + k, n)
        send_values(j).wait_send()
        send_keys(j).wait_send()

    @pl.loop(1, n)
    def _(k):
        recv_values(lax.rem(me + n - k, n)).wait_recv()


def body(mesh, fresh_keys, fresh_values, turn_angle):
    spans = mesh.shape["span"]
    n = mesh.shape["block"] * spans
    batch, length, heads, size = fresh_keys.shape
    seqs = batch // n
    rows = length * heads
    pages = length // PAGE
    flat = (batch, rows, size)
    hbm = pl.BlockSpec(memory_space=pltpu.HBM)
    vmem = pl.BlockSpec(memory_space=pltpu.VMEM)
    keys, values, high, low = pl.pallas_call(
        functools.partial(kernel, (spans, n, seqs, length, heads, size)),
        out_shape=(
            jax.ShapeDtypeStruct((seqs, heads, size, n * length), jnp.bfloat16),
            jax.ShapeDtypeStruct((seqs, n, rows, size), jnp.bfloat16),
            jax.ShapeDtypeStruct((seqs, n, pages * heads, size), jnp.bfloat16),
            jax.ShapeDtypeStruct((seqs, n, pages * heads, size), jnp.bfloat16),
        ),
        in_specs=[hbm] * 3,
        out_specs=(hbm, hbm, vmem, vmem),
        scratch_shapes=[
            pltpu.VMEM(flat, jnp.bfloat16),
            pltpu.VMEM(flat, jnp.bfloat16),
            pltpu.VMEM((rows, size), jnp.float32),
            pltpu.VMEM((rows, size), jnp.float32),
            pltpu.VMEM((rows, size), jnp.float32),
            pltpu.VMEM((size // 2, length), jnp.float32),
            pltpu.VMEM((2, heads, size, length), jnp.bfloat16),
            pltpu.VMEM((2, pages * heads, size), jnp.float32),
            pltpu.VMEM((seqs, rows, size), jnp.bfloat16),
            pltpu.SemaphoreType.DMA((n,)),
            pltpu.SemaphoreType.DMA((n,)),
            pltpu.SemaphoreType.DMA((n,)),
            pltpu.SemaphoreType.DMA((n,)),
            pltpu.SemaphoreType.DMA((2,)),
            pltpu.SemaphoreType.DMA((2,)),
            pltpu.SemaphoreType.DMA((2,)),
        ],
        compiler_params=pltpu.CompilerParams(
            collective_id=0, has_side_effects=True, vmem_limit_bytes=60 * 1024 * 1024
        ),
        name="exchange",
    )(fresh_keys.reshape(flat), fresh_values.reshape(flat), turn_angle.T)
    return (
        keys,
        values.reshape(seqs, n * length, heads, size),
        high.reshape(seqs, n * pages, heads, size),
        low.reshape(seqs, n * pages, heads, size),
    )


def solution(mesh):
    placed = (
        P(None, ("block", "span"), "model", None),
        P(None, ("block", "span"), "model", None),
        P(),
    )
    return jax.shard_map(
        functools.partial(body, mesh),
        mesh=mesh,
        in_specs=placed,
        out_specs=(
            P(("block", "span"), "model", None, None),
            P(("block", "span"), None, "model", None),
            P(("block", "span"), None, "model", None),
            P(("block", "span"), None, "model", None),
        ),
        check_vma=False,
    )
```

time: 419 us -> 386 us (0.921); the launches traced: 414 us -> 386 us
  Pallas kernels: 0 us -> 368 us
  blocking collectives: 189 us -> 0 us
  waiting for transfers between devices: 148 us -> 0 us
  other arithmetic: 46.1 us -> 0 us
  starting transfers between devices: 6.51 us -> 0 us
  local copies, waits for them, and re-layouts: 23.3 us -> 17.2 us
    pallas_call x0 -> x1, Pallas kernels: none -> 368 us  [body(): pl.pallas_call(functools.partial(kernel, (spans, n, seqs, length, heads,...]
    all_to_all x1 -> x0, blocking collectives: 189 us -> none  [body(): lax.all_to_all(sent_keys, ('block', 'span'), split_axis=0, concat_axis=1,...]
    all_to_all x1 -> x0, waiting for transfers between devices: 148 us -> none  [body(): lax.all_to_all(fresh_values, ('block', 'span'), split_axis=0, concat_axis...]
    reduce_min x1 -> x0, other arithmetic: 18.3 us -> none  [body(): page_low = jnp.min(page_view, axis=2)]
    all_to_all x1 -> x0, local copies, waits for them, and re-layouts: 13.6 us -> none  [body(): lax.all_to_all(sent_keys, ('block', 'span'), split_axis=0, concat_axis=1,...]
    another operation x1 -> x0, other arithmetic: 11.6 us -> none
    concatenate x1 -> x0, other arithmetic: 11.5 us -> none  [apply_rotary(): jnp.concatenate([first * cosine - second * sine, second * cosine + first...]
    unnamed x1 -> x8, local copies, waits for them, and re-layouts: 8.05 us -> 17.2 us
  transfers between devices with their start and end apart: 1 -> 0, of which waited for: 1 -> 0; matrix products, arithmetic and copies ran while one was open for 8% -> 0% of each run, Pallas kernels for 0% -> 0%
where the time goes in v1:
time: 386 us
  Pallas kernels  368 us (95%)
  local copies, waits for them, and re-layouts  17.2 us (4%)
    pallas_call x1, Pallas kernels, body(): pl.pallas_call(functools.partial(kernel, (spans, n, seqs, length, heads,...  368 us
    unnamed x8, local copies, waits for them, and re-layouts  17.2 us

profile of v1, /device:TPU:9, one launch (start us, length us, event | category | flops | bytes accessed | tf_op | source)
XLA Modules:
  0.0 385.9 jit_solution(17218086860648372946)
XLA Ops:
  0.6 368.1 %exchange.1 = (bf16[1,4,128,8192]{3,2,1,0:T(8,128)(2,1)}, bf16[1,16,2048,128]{3,2,1,0:T(8,128)(2,1)}, bf16[1,16,32,128]{3,2,1,0:T(8,128)(2,1)}, bf16[1,16,32,128]{3,2,1,0:T(8,128)(2,1)}) custom-call(bf16[16,2048,128]{2,1,0:T(8,128)(2,1)} %bitcast.6, bf16[16,2048,128]{2,1,0:T(8,128)(2,1)} %bitcast.7, f32[64,8192]{1,0:T(8,128)} %bitcast.9), custom_call_target="tpu_custom_call" | custom-call | tf_op jit(solution)/shard_map/exchange/pallas_call | solution.py:184
  368.8 7.8 %copy.11 = bf16[1,4,128,8192]{3,2,1,0:T(8,128)(2,1)} copy(bf16[1,4,128,8192]{3,2,1,0:T(8,128)(2,1)} %get-tuple-element.16) | data formatting | bytes 16777216
  376.5 0.0 copy-start.1
  376.5 0.0 copy-start
  376.5 8.1 %copy.12 = bf16[1,8192,4,128]{3,2,1,0:T(4,128)(2,1)} copy(bf16[1,8192,4,128]{3,2,1,0:T(4,128)(2,1)} %bitcast.8) | data formatting | bytes 16777216
  384.6 0.0 copy-done.1
  384.6 0.7 copy.13
  385.3 0.0 copy-done
  385.3 0.7 copy.14
Async XLA Ops:
  376.5 8.1 %copy-start.1 = (bf16[1,16,32,128]{3,2,1,0:T(8,128)(2,1)S(1)}, bf16[1,16,32,128]{3,2,1,0:T(8,128)(2,1)}, u32[]{:S(2)}) copy-start(bf16[1,16,32,128]{3,2,1,0:T(8,128)(2,1)} %get-tuple-element.10) | copy-start | bytes 393220
  376.5 8.8 %copy-start = (bf16[1,16,32,128]{3,2,1,0:T(8,128)(2,1)S(1)}, bf16[1,16,32,128]{3,2,1,0:T(8,128)(2,1)}, u32[]{:S(2)}) copy-start(bf16[1,16,32,128]{3,2,1,0:T(8,128)(2,1)} %get-tuple-element.11) | copy-start | bytes 393220

commit v2 on v1

--- a/solution.py
+++ b/solution.py
@@ -9,17 +9,19 @@
 
 PAGE = 64
 ROWS = 256
+TAIL = 8
 
 
 def kernel(
     dims, keys, values, angle,
-    out_keys, out_values, out_high, out_low,
-    held, landed, wide, cosine, sine, turn, staged, bounds, own,
+    out_keys, out_values, out_high, out_low, out_late,
+    held, landed, wide, cosine, sine, turn, staged, bounds, own, late,
     send_v, recv_v, send_k, recv_k, load_sem, own_sem, stage_sem,
 ):
     spans, n, seqs, length, heads, size = dims
     rows = length * heads
     pages = length // PAGE
+    most = rows - rows // TAIL
     block, span, model = (lax.axis_index(a) for a in ("block", "span", "model"))
     me = block * spans + span
 
@@ -28,7 +30,7 @@
 
     def send_values(j):
         return pltpu.make_async_remote_copy(
-            src_ref=values.at[pl.ds(j * seqs, seqs)],
+            src_ref=values.at[pl.ds(j * seqs, seqs), pl.ds(0, most)],
             dst_ref=out_values.at[:, me],
             send_sem=send_v.at[j],
             recv_sem=recv_v.at[me],
@@ -38,7 +40,7 @@
 
     def recv_values(j):
         return pltpu.make_async_remote_copy(
-            src_ref=values.at[pl.ds(j * seqs, seqs)],
+            src_ref=values.at[pl.ds(j * seqs, seqs), pl.ds(0, most)],
             dst_ref=out_values.at[:, j],
             send_sem=send_v.at[j],
             recv_sem=recv_v.at[j],
@@ -70,11 +72,17 @@
     load_angle = pltpu.make_async_copy(
         angle.at[:, pl.ds(pl.multiple_of(me * length, length), length)], turn, load_sem.at[1]
     )
-    load_own = pltpu.make_async_copy(values.at[pl.ds(me * seqs, seqs)], own, own_sem.at[0])
+    load_own = pltpu.make_async_copy(values.at[pl.ds(me * seqs, seqs), pl.ds(0, most)], own, own_sem.at[0]
+    )
     keep_own = pltpu.make_async_copy(own, out_values.at[:, me], own_sem.at[1])
+    load_late = pltpu.make_async_copy(
+        values.at[:, pl.ds(most, rows - most)], late, own_sem.at[2]
+    )
+    keep_late = pltpu.make_async_copy(late, out_late, own_sem.at[3])
     load_angle.start()
     load_keys.start()
     load_own.start()
+    load_late.start()
 
     barrier = pltpu.get_barrier_semaphore()
 
@@ -100,6 +108,8 @@
         sine[pl.ds(h, length, stride=heads), :] = wide_s
     load_own.wait()
     keep_own.start()
+    load_late.wait()
+    keep_late.start()
     load_keys.wait()
 
     def rotate(j):
@@ -120,6 +130,7 @@
         send_keys(lax.rem(me + k - 1, n)).start()
 
     keep_own.wait()
+    keep_late.wait()
 
     def stage(j, q, slot):
         return pltpu.make_async_copy(
@@ -169,6 +180,15 @@
     @pl.loop(1, n)
     def _(k):
         recv_values(lax.rem(me + n - k, n)).wait_recv()
+
+
+def copy_kernel(keys, values, out_keys, out_values):
+    out_keys[...] = keys[...]
+    out_values[...] = values[...]
+
+
+def late_kernel(_, late, out):
+    out[...] = late[...]
 
 
 def body(mesh, fresh_keys, fresh_values, turn_angle):
@@ -181,16 +201,18 @@
     flat = (batch, rows, size)
     hbm = pl.BlockSpec(memory_space=pltpu.HBM)
     vmem = pl.BlockSpec(memory_space=pltpu.VMEM)
-    keys, values, high, low = pl.pallas_call(
+    most = rows - rows // TAIL
+    keys, values, high, low, late = pl.pallas_call(
         functools.partial(kernel, (spans, n, seqs, length, heads, size)),
         out_shape=(
             jax.ShapeDtypeStruct((seqs, heads, size, n * length), jnp.bfloat16),
-            jax.ShapeDtypeStruct((seqs, n, rows, size), jnp.bfloat16),
+            jax.ShapeDtypeStruct((seqs, n, most, size), jnp.bfloat16),
             jax.ShapeDtypeStruct((seqs, n, pages * heads, size), jnp.bfloat16),
             jax.ShapeDtypeStruct((seqs, n, pages * heads, size), jnp.bfloat16),
+            jax.ShapeDtypeStruct((batch, rows - most, size), jnp.bfloat16),
         ),
         in_specs=[hbm] * 3,
-        out_specs=(hbm, hbm, vmem, vmem),
+        out_specs=(hbm, hbm, vmem, vmem, hbm),
         scratch_shapes=[
             pltpu.VMEM(flat, jnp.bfloat16),
             pltpu.VMEM(flat, jnp.bfloat16),
@@ -200,13 +222,14 @@
             pltpu.VMEM((size // 2, length), jnp.float32),
             pltpu.VMEM((2, heads, size, length), jnp.bfloat16),
             pltpu.VMEM((2, pages * heads, size), jnp.float32),
-            pltpu.VMEM((seqs, rows, size), jnp.bfloat16),
+            pltpu.VMEM((seqs, most, size), jnp.bfloat16),
+            pltpu.VMEM((batch, rows - most, size), jnp.bfloat16),
             pltpu.SemaphoreType.DMA((n,)),
             pltpu.SemaphoreType.DMA((n,)),
             pltpu.SemaphoreType.DMA((n,)),
             pltpu.SemaphoreType.DMA((n,)),
             pltpu.SemaphoreType.DMA((2,)),
-            pltpu.SemaphoreType.DMA((2,)),
+            pltpu.SemaphoreType.DMA((4,)),
             pltpu.SemaphoreType.DMA((2,)),
         ],
         compiler_params=pltpu.CompilerParams(
@@ -214,6 +237,40 @@
         ),
         name="exchange",
     )(fresh_keys.reshape(flat), fresh_values.reshape(flat), turn_angle.T)
+    late = lax.all_to_all(late, ("block", "span"), split_axis=0, concat_axis=0, tiled=True)
+    late = jnp.swapaxes(late.reshape(n, seqs, rows - most, size), 0, 1)
+    keys, values = pl.pallas_call(
+        copy_kernel,
+        grid=(seqs, n),
+        out_shape=(
+            jax.ShapeDtypeStruct(keys.shape, keys.dtype),
+            jax.ShapeDtypeStruct((seqs, n, rows, size), jnp.bfloat16),
+        ),
+        in_specs=[
+            pl.BlockSpec((1, heads, size, length), lambda q, j: (q, 0, 0, j)),
+            pl.BlockSpec((1, 1, most, size), lambda q, j: (q, j, 0, 0)),
+        ],
+        out_specs=(
+            pl.BlockSpec((1, heads, size, length), lambda q, j: (q, 0, 0, j)),
+            pl.BlockSpec((1, 1, most, size), lambda q, j: (q, j, 0, 0)),
+        ),
+        cost_estimate=pl.CostEstimate(
+            flops=0, bytes_accessed=8 * seqs * n * rows * size, transcendentals=0
+        ),
+        name="keep",
+    )(keys, values)
+    values = pl.pallas_call(
+        late_kernel,
+        grid=(seqs, n),
+        out_shape=jax.ShapeDtypeStruct(values.shape, values.dtype),
+        in_specs=[
+            pl.BlockSpec(memory_space=pltpu.HBM),
+            pl.BlockSpec((1, 1, rows - most, size), lambda q, j: (q, j, 0, 0)),
+        ],
+        out_specs=pl.BlockSpec((1, 1, rows - most, size), lambda q, j: (q, j, TAIL - 1, 0)),
+        input_output_aliases={0: 0},
+        name="join",
+    )(values, late)
     return (
         keys,
         values.reshape(seqs, n * length, heads, size),

time: 386 us -> 392 us (1.016); the launches traced: 386 us -> 387 us
  local copies, waits for them, and re-layouts: 17.2 us -> 2.29 us
  waiting for transfers between devices: 0 us -> 6.88 us
  starting transfers between devices: 0 us -> 5.76 us
    pallas_call x0 -> x2, Pallas kernels: none -> 25.5 us  [the longest x1 16.6 us: body(): pl.pallas_call(copy_kernel, grid=(seqs, n), out_shape=(jax.ShapeDtypeStru...]
    pallas_call x1, Pallas kernels: 368 us -> 346 us  [body(): pl.pallas_call(functools.partial(kernel, (spans, n, seqs, length, heads,...]
    unnamed x8, local copies, waits for them, and re-layouts: 17.2 us -> 2.29 us
    all_to_all x0 -> x1, waiting for transfers between devices: none -> 6.88 us  [body(): lax.all_to_all(late, ('block', 'span'), split_axis=0, concat_axis=0, tile...]
    all_to_all x0 -> x1, starting transfers between devices: none -> 5.76 us  [body(): lax.all_to_all(late, ('block', 'span'), split_axis=0, concat_axis=0, tile...]
  transfers between devices with their start and end apart: 0 -> 1, of which waited for: 0 -> 1; matrix products, arithmetic and copies ran while one was open for 0% -> 0% of each run, Pallas kernels for 0% -> 4%
where the time goes in v2:
time: 392 us; the launch traced here: 387 us
  Pallas kernels  371 us (95%)
  waiting for transfers between devices  6.88 us (2%)
  starting transfers between devices  5.76 us (1%)
    pallas_call x1, Pallas kernels, body(): pl.pallas_call(functools.partial(kernel, (spans, n, seqs, length, heads,...  346 us
    pallas_call x1, Pallas kernels, body(): pl.pallas_call(copy_kernel, grid=(seqs, n), out_shape=(jax.ShapeDtypeStru...  16.6 us
    pallas_call x1, Pallas kernels, body(): pl.pallas_call(late_kernel, grid=(seqs, n), out_shape=jax.ShapeDtypeStruc...  8.9 us
  transfers between devices with their start and end apart: 1, of which 1 were waited for; matrix products, arithmetic and copies ran while one was open for 0% of the time, Pallas kernels for 4%

profile of v2, /device:TPU:9, one launch (start us, length us, event | category | flops | bytes accessed | tf_op | source)
XLA Modules:
  0.0 386.9 jit_solution(3750649367926789231)
XLA Ops:
  0.6 345.8 %exchange.1 = (bf16[1,4,128,8192]{3,2,1,0:T(8,128)(2,1)}, bf16[1,16,1792,128]{3,2,1,0:T(8,128)(2,1)}, bf16[1,16,32,128]{3,2,1,0:T(8,128)(2,1)}, bf16[1,16,32,128]{3,2,1,0:T(8,128)(2,1)}, bf16[16,256,128]{2,1,0:T(8,128)(2,1)}) custom-call(bf16[16,2048,128]{2,1,0:T(8,128)(2,1)} %bitcast.7, bf16[16,2048,128]{2,1,0:T(8,128)(2,1)} %bitcast.8, f32[64,8192]{1,0:T(8,128)} %bitcast.11), custom_call_target="tpu_custom_call" | custom-call | tf_op jit(solution)/shard_map/exchange/pallas_call | solution.py:205
  346.4 5.8 %all-to-all-start = ((bf16[16,256,128]{2,1,0:T(8,128)(2,1)}), bf16[16,256,128]{2,1,0:T(8,128)(2,1)S(1)}, u32[]{:S(2)}, u32[]{:S(2)}) async-start(bf16[16,256,128]{2,1,0:T(8,128)(2,1)} %get-tuple-element.15), calls=%async_computation | async-start | bytes 2097152 | tf_op jit(solution)/shard_map/all_to_all | solution.py:240
  352.2 16.6 %keep.1 = (bf16[1,4,128,8192]{3,2,1,0:T(8,128)(2,1)}, bf16[1,16,2048,128]{3,2,1,0:T(8,128)(2,1)}) custom-call(bf16[1,4,128,8192]{3,2,1,0:T(8,128)(2,1)} %get-tuple-element.11.keys, bf16[1,16,1792,128]{3,2,1,0:T(8,128)(2,1)} %get-tuple-element.12.values), custom_call_target="tpu_custom_call" | custom-call | bytes 33554432 | tf_op jit(solution)/shard_map/keep/pallas_call | solution.py:242
  368.8 6.9 %all-to-all-done = bf16[16,256,128]{2,1,0:T(8,128)(2,1)S(1)} async-done(((bf16[16,256,128]{2,1,0:T(8,128)(2,1)}), bf16[16,256,128]{2,1,0:T(8,128)(2,1)S(1)}, u32[]{:S(2)}, u32[]{:S(2)}) %all-to-all-start) | async-done | bytes 1048608 | tf_op jit(solution)/shard_map/all_to_all | solution.py:240
  375.7 0.0 copy-start
  375.7 1.0 copy-done
  376.6 0.0 copy-start.2
  376.7 0.0 copy-start.1
  376.7 8.9 %join.1 = bf16[1,16,2048,128]{3,2,1,0:T(8,128)(2,1)} custom-call(bf16[1,16,2048,128]{3,2,1,0:T(8,128)(2,1)} %get-tuple-element.14._, bf16[1,16,256,128]{3,2,1,0:T(8,128)(2,1)} %bitcast.10), custom_call_target="tpu_custom_call", output_to_operand_aliasing={{}: (0, {})} | custom-call | tf_op jit(solution)/shard_map/join/pallas_call | solution.py:262
  385.6 0.0 copy-done.2
  385.6 0.7 copy.11
  386.2 0.0 copy-done.1
  386.2 0.7 copy.12
Async XLA Ops:
  346.4 29.3 %all-to-all-start = ((bf16[16,256,128]{2,1,0:T(8,128)(2,1)}), bf16[16,256,128]{2,1,0:T(8,128)(2,1)S(1)}, u32[]{:S(2)}, u32[]{:S(2)}) async-start(bf16[16,256,128]{2,1,0:T(8,128)(2,1)} %get-tuple-element.15), calls=%async_computation | async-start | bytes 2097152 | tf_op jit(solution)/shard_map/all_to_all | solution.py:240
  375.7 1.0 copy-start
  376.6 8.9 %copy-start.2 = (bf16[1,16,32,128]{3,2,1,0:T(8,128)(2,1)S(1)}, bf16[1,16,32,128]{3,2,1,0:T(8,128)(2,1)}, u32[]{:S(2)}) copy-start(bf16[1,16,32,128]{3,2,1,0:T(8,128)(2,1)} %get-tuple-element.16) | copy-start | bytes 393220
  376.7 9.6 %copy-start.1 = (bf16[1,16,32,128]{3,2,1,0:T(8,128)(2,1)S(1)}, bf16[1,16,32,128]{3,2,1,0:T(8,128)(2,1)}, u32[]{:S(2)}) copy-start(bf16[1,16,32,128]{3,2,1,0:T(8,128)(2,1)} %get-tuple-element.17) | copy-start | bytes 393220
